TPU v7x, 32 devices: a whole 2x2x4 slice. The times are simulated.
32 devices in a mesh: freq: 4 (over y, x), space: 8 (over z, core).
Axes of the slice: x: 2, y: 2, z: 4, core: 2. Of those that a mesh axis runs over, the one named last changes fastest.
Arguments:
- spectra: bfloat16 [64, 24576, 256], P('freq', 'space'), may hold values from -48 to 48, as said below
- weight: float32 [24576], P('space'), may hold values from 0.25 to 4
- partner: int32 [64], P('freq'), may hold values from 0 to 15
- counts: int32 [64], P('freq'), may hold values from 1 to 8
Outputs:
- modes: bfloat16 [64, 16, 24576], P('freq', None, 'space')
- energy: float32 [64, 8], P('freq')
- coherence: float32 [64, 2, 8, 8], P('freq')
Inputs may be any that keep to these rules, and one draw needn't show every extreme that they name: spectra are finite Fourier coefficients.
All inputs are finite; a program needn't handle non-finite values.
Results may differ from a plain program's by a relative error of at most 0.0045.
Values may be sent and summed in bfloat16 or wider, within the bound.
A program may use at most 128 MiB of HBM per device.

v0:
```python
import jax
import jax.numpy as jnp
from jax import lax
from jax.sharding import PartitionSpec as P

KMAX = 8
ITERS = 4


def from_partner(block, axis, apart):
    count = lax.axis_size(axis)
    route = []
    for low in range(count):
        high = low | 1 << apart
        if high != low and high < count:
            route += [(low, high), (high, low)]
    return lax.ppermute(block, axis, route)


def embed(gram_re, gram_im):
    top = jnp.concatenate([gram_re, -gram_im], axis=2)
    bottom = jnp.concatenate([gram_im, gram_re], axis=2)
    return jnp.concatenate([top, bottom], axis=1)


def apply_operator(operator, basis):
    return jnp.einsum("fkc,fdc->fkd", basis, operator, precision=lax.Precision.HIGHEST)


def orthonormal(vectors, half):
    done = []
    for index in range(vectors.shape[1]):
        vector = vectors[:, index, :]
        for earlier in done:
            early_re, early_im = (earlier[:, :half], earlier[:, half:])
            vec_re, vec_im = (vector[:, :half], vector[:, half:])
            proj_re = jnp.sum(early_re * vec_re + early_im * vec_im, axis=1, keepdims=True)
            proj_im = jnp.sum(early_re * vec_im - early_im * vec_re, axis=1, keepdims=True)
            new_re = vec_re - proj_re * early_re + proj_im * early_im
            new_im = vec_im - proj_re * early_im - proj_im * early_re
            vector = jnp.concatenate([new_re, new_im], axis=1)
        length = jnp.sqrt(jnp.sum(vector * vector, axis=1, keepdims=True) + 1e-06)
        done.append(vector / length)
    return jnp.stack(done, axis=1)


def solve(gram_re, gram_im):
    half = gram_re.shape[1]
    operator = embed(gram_re, gram_im)
    basis = jnp.broadcast_to(
        jnp.eye(KMAX, 2 * half, dtype=jnp.float32), (gram_re.shape[0], KMAX, 2 * half)
    )
    for sweep in range(ITERS):
        basis = orthonormal(apply_operator(operator, basis), half)
    image = apply_operator(operator, basis)
    energy = jnp.sum(basis * image, axis=2)
    return (basis, energy)


def combine(moments, half, total):
    gram_re = (moments[:, :half, :half] + moments[:, half:, half:]) / total
    gram_im = (moments[:, :half, half:] - moments[:, half:, :half]) / total
    return (gram_re, gram_im)


def coefficients(basis, energy, counts):
    half = basis.shape[2] // 2
    ranks = jnp.arange(KMAX, dtype=jnp.int32)[None, :]
    scale = jnp.where(ranks < counts[:, None], 1.0 / jnp.sqrt(energy + 1e-06), 0.0)[:, :, None]
    part_re, part_im = (basis[:, :, :half], basis[:, :, half:])
    upper = jnp.concatenate([part_re, -part_im], axis=2) * scale
    lower = jnp.concatenate([part_im, part_re], axis=2) * scale
    return jnp.concatenate([upper, lower], axis=1).astype(jnp.bfloat16)


def cross_terms(own_modes, other_modes, point_weight, total):
    phi = own_modes.astype(jnp.float32)
    psi = other_modes.astype(jnp.float32)
    wphi = phi * point_weight[None, None, :]
    highest = lax.Precision.HIGHEST

    def inner(left, right):
        return jnp.einsum("fkp,flp->fkl", left, right, precision=highest)

    real_part = inner(wphi[:, :KMAX], psi[:, :KMAX]) + inner(wphi[:, KMAX:], psi[:, KMAX:])
    imag_part = inner(wphi[:, :KMAX], psi[:, KMAX:]) - inner(wphi[:, KMAX:], psi[:, :KMAX])
    return jnp.stack([real_part, imag_part], axis=1) / total


def on_device(spectra, weight, partner, counts):
    groups = spectra.shape[0]
    half = spectra.shape[2] // 2
    total = spectra.shape[1] * lax.axis_size("space")
    weighted = (weight[None, :, None] * spectra).astype(jnp.bfloat16)
    moments = lax.dot_general(
        spectra, weighted, (((1,), (1,)), ((0,), (0,))), preferred_element_type=jnp.float32
    )
    summed = lax.psum(moments, "space")
    gram_re, gram_im = combine(summed, half, total)
    basis, energy = solve(gram_re, gram_im)
    coefficient = coefficients(basis, energy, counts)
    modes = jnp.einsum(
        "fkc,fpc->fkp", coefficient, spectra, preferred_element_type=jnp.float32
    ).astype(jnp.bfloat16)
    levels = lax.axis_size("freq").bit_length() - 1
    mirrored = modes
    for bit in range(levels):
        mirrored = from_partner(mirrored, "freq", bit)
    match = (partner[:, None] == jnp.arange(groups, dtype=jnp.int32)[None, :]).astype(jnp.bfloat16)
    chosen = jnp.einsum("fg,gkp->fkp", match, mirrored, preferred_element_type=jnp.float32).astype(
        jnp.bfloat16
    )
    local = cross_terms(modes, chosen, weight, total)
    coherence = lax.psum(local, "space")
    return (modes, energy, coherence)


def solution(mesh):
    in_specs = (P("freq", "space", None), P("space"), P("freq"), P("freq"))
    out_specs = (P("freq", None, "space"), P("freq", None), P("freq", None, None, None))
    return jax.shard_map(
        on_device, mesh=mesh, in_specs=in_specs, out_specs=out_specs, check_vma=False
    )
```

profile of v0, /device:TPU:0, one launch (start us, length us, event | category | flops | bytes accessed | tf_op | source)
XLA Modules:
  0.0 290.2 jit_solution(2149110146235932898)
XLA Ops:
  7.2 20.7 %fusion.2 = f32[16,256,256]{1,2,0:T(8,128)} fusion(bf16[16,3072,256]{2,1,0:T(8,128)(2,1)} %param.4, f32[3072]{0:T(1024)} %param.5), kind=kOutput, calls=%fused_computation.7 | convolution fusion | flops 6480199680 | bytes 29372416 | tf_op jit(solution)/shard_map/dot_general | solution.py:95
  27.9 99.3 %all-reduce.2.cloned.1.call-done = f32[16,256,256]{1,2,0:T(8,128)} async-done(((f32[16,256,256]{1,2,0:T(8,128)}), f32[16,256,256]{1,2,0:T(8,128)}) %all-reduce.2.cloned.1.call-update) | async-done | bytes 4194320 | tf_op jit(solution)/shard_map/psum | solution.py:98
  127.2 2.8 fusion.80
  130.0 1.9 fusion.42
  132.7 0.3 add_reduce_fusion.96
  133.6 0.3 add_reduce_fusion.89
  134.4 0.3 add_reduce_fusion.88
  135.1 0.3 add_reduce_fusion.87
  137.4 2.0 fusion.40
  140.2 0.3 add_reduce_fusion.68
  141.1 0.3 add_reduce_fusion.61
  142.7 0.3 add_reduce_fusion.59
  145.0 2.0 fusion.38
  147.8 0.3 add_reduce_fusion.40
  148.6 0.3 add_reduce_fusion.33
  150.2 0.3 add_reduce_fusion.31
  152.5 2.2 fusion.36
  155.5 0.3 add_reduce_fusion.12
  156.4 0.3 add_reduce_fusion.5
  160.3 2.0 fusion.34
  162.5 12.4 %convert_multiply_fusion = (f32[16,16,3072]{2,1,0:T(8,128)S(1)}, bf16[16,16,3072]{2,1,0:T(8,128)(2,1)}) fusion(f32[3072]{0:T(1024)S(1)} %copy-done, bf16[16,3072,256]{2,1,0:T(8,128)(2,1)} %param.4, bf16[16,16,256]{2,0,1:T(8,128)(2,1)S(1)} %pad_maximum_fusion), kind=kOutput, calls=%fused_computation.6 | convolution fusion | flops 405012480 | bytes 30027776 | tf_op jit(solution)/shard_map/fkc,fpc->fkp/dot_general | solution.py:102
  175.0 1.5 collective-permute-start
  176.5 34.6 %collective-permute-done = bf16[16,16,3072]{2,1,0:T(8,128)(2,1)S(1)} collective-permute-done((bf16[16,16,3072]{2,1,0:T(8,128)(2,1)}, bf16[16,16,3072]{2,1,0:T(8,128)(2,1)S(1)}, u32[]{:S(2)}, u32[]{:S(2)}) %collective-permute-start) | collective-permute-done | bytes 1572896 | tf_op jit(solution)/shard_map/ppermute | solution.py:17
  211.1 1.5 collective-permute-start.1
  212.6 33.6 %collective-permute-done.1 = bf16[16,16,3072]{2,1,0:T(8,128)(2,1)S(1)} collective-permute-done((bf16[16,16,3072]{2,1,0:T(8,128)(2,1)S(1)}, bf16[16,16,3072]{2,1,0:T(8,128)(2,1)S(1)}, u32[]{:S(2)}, u32[]{:S(2)}) %collective-permute-start.1) | collective-permute-done | bytes 1572896 | tf_op jit(solution)/shard_map/ppermute | solution.py:17
  246.1 1.9 convolution_convert_fusion
  248.1 1.8 fusion.6
  249.9 1.8 fusion.4
  251.7 1.5 fusion.15
  253.2 1.8 fusion.21
  255.0 27.5 %psum.15 = f32[16,2,8,8]{3,2,0,1:T(8,128)S(1)} all-reduce(f32[16,2,8,8]{3,2,0,1:T(8,128)S(1)} %maximum_multiply_fusion.2), channel_id=1, replica_groups=mesh['freq'=4,'space'=8] {'space'}, use_global_device_ids=true, to_apply=%region_258.259 | all-reduce | flops 2048 | bytes 16384 | tf_op jit(solution)/shard_map/psum | solution.py:114
  282.6 0.7 copy.52
  (231 shorter events, 18.9 us)
Async XLA Ops:
  7.2 120.1 %all-reduce.2.cloned.1.call-start = ((), (), s32[]{:S(2)}) async-start(), calls=%async_computation | async-start | bytes 8388608 | tf_op jit(solution)/shard_map/psum | solution.py:98
  158.5 3.9 %copy-start.2 = (s32[16]{0:T(128)S(1)}, s32[16]{0:T(128)}, u32[]{:S(2)}) copy-start(s32[16]{0:T(128)} %param.7) | copy-start | bytes 196
  160.0 2.6 copy-start
  162.4 12.6 %copy-start.1 = (f32[16,8]{0,1:T(8,128)}, f32[16,8]{0,1:T(8,128)S(1)}, u32[]{:S(2)}) copy-start(f32[16,8]{0,1:T(8,128)S(1)} %fusion.33) | copy-start | bytes 1540
  162.5 83.6 %copy-start.3 = (s32[16]{0:T(128)S(1)}, s32[16]{0:T(128)}, u32[]{:S(2)}) copy-start(s32[16]{0:T(128)} %param.6) | copy-start | bytes 196
  175.0 36.1 %collective-permute-start = (bf16[16,16,3072]{2,1,0:T(8,128)(2,1)}, bf16[16,16,3072]{2,1,0:T(8,128)(2,1)S(1)}, u32[]{:S(2)}, u32[]{:S(2)}) collective-permute-start(bf16[16,16,3072]{2,1,0:T(8,128)(2,1)} %get-tuple-element.649), channel_id=1, source_target_pairs={{0,8},{8,0},{16,24},{24,16},{1,9},{9,1},{17,25},{25,17},{2,10},{10... | collective-permute-start | bytes 4718600 | tf_op jit(solution)/shard_map/ppermute | solution.py:17
  211.1 35.0 %collective-permute-start.1 = (bf16[16,16,3072]{2,1,0:T(8,128)(2,1)S(1)}, bf16[16,16,3072]{2,1,0:T(8,128)(2,1)S(1)}, u32[]{:S(2)}, u32[]{:S(2)}) collective-permute-start(bf16[16,16,3072]{2,1,0:T(8,128)(2,1)S(1)} %collective-permute-done), channel_id=1, source_target_pairs={{0,16},{16,0},{8,24},{24,8},{1,17},{17,1},{9,25},{25,9},{2,18},{18... | collective-permute-start | bytes 4718600 | tf_op jit(solution)/shard_map/ppermute | solution.py:17
Sparse Core Ops, SparseCore 0:
  28.0 99.1 all-reduce.1
where the time goes:
time: 290 us
  waiting for transfers between devices  168 us (58%)
  matrix products  51.8 us (18%)
  blocking collectives  27.5 us (9%)
  other arithmetic  24.4 us (8%)
  between operations  14.6 us (5%)
  starting transfers between devices  2.98 us (1%)
    psum x1, waiting for transfers between devices, on_device(): summed = lax.psum(moments, 'space')  99.3 us
    ppermute x2, waiting for transfers between devices, from_partner(): return lax.ppermute(block, axis, route)  68.2 us
    psum x1, blocking collectives, on_device(): coherence = lax.psum(local, 'space')  27.5 us
    dot_general x1, matrix products, on_device(): lax.dot_general(spectra, weighted, (((1,), (1,)), ((0,), (0,))), preferre...  20.7 us
    dot_general x1, matrix products, on_device(): jnp.einsum('fkc,fpc->fkp', coefficient, spectra, preferred_element_type=j...  12.4 us
    reduce_sum x44, other arithmetic, orthonormal(): jnp.sum(early_re * vec_re + early_im * vec_im, axis=1, keepdims=True)  10.6 us
    dot_general x5, matrix products, apply_operator(): jnp.einsum('fkc,fdc->fkd', basis, operator, precision=lax.Precision.HIGHEST)  9.94 us
    dot_general x4, matrix products, inner(): return jnp.einsum('fkp,flp->fkl', left, right, precision=highest)  6.86 us
  transfers between devices with their start and end apart: 3, of which 3 were waited for; matrix products, arithmetic and copies ran while one was open for 0% of the time, Pallas kernels for 0%

commit v1 on v0

--- a/solution.py
+++ b/solution.py
@@ -95,7 +95,11 @@
     moments = lax.dot_general(
         spectra, weighted, (((1,), (1,)), ((0,), (0,))), preferred_element_type=jnp.float32
     )
-    summed = lax.psum(moments, "space")
+    size = lax.axis_size("space")
+    summed, far = (moments, 1)
+    while far < size:
+        summed = summed + lax.ppermute(summed, "space", [(i, i ^ far) for i in range(size)])
+        far = 2 * far
     gram_re, gram_im = combine(summed, half, total)
     basis, energy = solve(gram_re, gram_im)
     coefficient = coefficients(basis, energy, counts)

time: 290 us -> 465 us (1.60)
  waiting for transfers between devices: 168 us -> 345 us
  between operations: 14.6 us -> 1.2 us
  starting transfers between devices: 2.98 us -> 8.97 us
    ppermute x0 -> x3, waiting for transfers between devices: none -> 278 us  [on_device(): lax.ppermute(summed, 'space', [(i, i ^ far) for i in range(size)])]
    psum x1 -> x0, waiting for transfers between devices: 99.3 us -> none  [on_device(): summed = lax.psum(moments, 'space')]
    ppermute x0 -> x3, starting transfers between devices: none -> 6.31 us  [on_device(): lax.ppermute(summed, 'space', [(i, i ^ far) for i in range(size)])]
  transfers between devices with their start and end apart: 3 -> 5, of which waited for: 3 -> 5; matrix products, arithmetic and copies ran while one was open for 0% -> 0% of each run, Pallas kernels for 0% -> 0%
where the time goes in v1:
time: 465 us
  waiting for transfers between devices  345 us (74%)
  matrix products  51.5 us (11%)
  blocking collectives  30.1 us (6%)
  other arithmetic  26.3 us (6%)
  starting transfers between devices  8.97 us (2%)
    ppermute x3, waiting for transfers between devices, on_device(): lax.ppermute(summed, 'space', [(i, i ^ far) for i in range(size)])  278 us
    ppermute x2, waiting for transfers between devices, from_partner(): return lax.ppermute(block, axis, route)  67.5 us
    psum x1, blocking collectives, on_device(): coherence = lax.psum(local, 'space')  30.1 us
    dot_general x1, matrix products, on_device(): lax.dot_general(spectra, weighted, (((1,), (1,)), ((0,), (0,))), preferre...  20.6 us
    dot_general x1, matrix products, on_device(): jnp.einsum('fkc,fpc->fkp', coefficient, spectra, preferred_element_type=j...  12.4 us
    reduce_sum x44, other arithmetic, orthonormal(): jnp.sum(early_re * vec_re + early_im * vec_im, axis=1, keepdims=True)  10.6 us
    dot_general x5, matrix products, apply_operator(): jnp.einsum('fkc,fdc->fkd', basis, operator, precision=lax.Precision.HIGHEST)  9.73 us
  transfers between devices with their start and end apart: 5, of which 5 were waited for; matrix products, arithmetic and copies ran while one was open for 0% of the time, Pallas kernels for 0%

profile of v1, /device:TPU:0, one launch (start us, length us, event | category | flops | bytes accessed | tf_op | source)
XLA Modules:
  0.0 465.2 jit_solution(6830693556247651348)
XLA Ops:
  0.6 20.6 %fusion.2 = f32[16,256,256]{1,2,0:T(8,128)} fusion(bf16[16,3072,256]{2,1,0:T(8,128)(2,1)} %param.4, f32[3072]{0:T(1024)} %param.5), kind=kOutput, calls=%fused_computation.7 | convolution fusion | flops 6480199680 | bytes 29372416 | tf_op jit(solution)/shard_map/dot_general | solution.py:95
  21.2 0.5 collective-permute-start
  21.7 7.0 %collective-permute-done = f32[16,256,256]{1,2,0:T(8,128)S(1)} collective-permute-done((f32[16,256,256]{1,2,0:T(8,128)}, f32[16,256,256]{1,2,0:T(8,128)S(1)}, u32[]{:S(2)}, u32[]{:S(2)}) %collective-permute-start) | collective-permute-done | bytes 4194336 | tf_op jit(solution)/shard_map/ppermute | solution.py:101
  28.7 3.0 add.955
  31.8 3.0 collective-permute-start.1
  34.8 90.9 %collective-permute-done.1 = f32[16,256,256]{1,2,0:T(8,128)S(1)} collective-permute-done((f32[16,256,256]{1,2,0:T(8,128)S(1)}, f32[16,256,256]{1,2,0:T(8,128)S(1)}, u32[]{:S(2)}, u32[]{:S(2)}) %collective-permute-start.1) | collective-permute-done | bytes 4194336 | tf_op jit(solution)/shard_map/ppermute | solution.py:101
  125.6 0.6 add.956
  126.3 2.8 collective-permute-start.2
  129.1 180.1 %collective-permute-done.2 = f32[16,256,256]{1,2,0:T(8,128)S(1)} collective-permute-done((f32[16,256,256]{1,2,0:T(8,128)S(1)}, f32[16,256,256]{1,2,0:T(8,128)S(1)}, u32[]{:S(2)}, u32[]{:S(2)}) %collective-permute-start.2) | collective-permute-done | bytes 4194336 | tf_op jit(solution)/shard_map/ppermute | solution.py:101
  309.2 0.6 add.957
  309.8 0.4 fusion.80
  310.2 1.9 fusion.42
  312.9 0.3 add_reduce_fusion.96
  317.6 2.0 fusion.40
  320.5 0.3 add_reduce_fusion.68
  325.2 2.0 fusion.38
  328.2 0.3 add_reduce_fusion.40
  332.9 2.0 fusion.36
  335.7 0.3 add_reduce_fusion.12
  340.5 2.0 fusion.34
  342.8 12.4 %convert_multiply_fusion = (f32[16,16,3072]{2,1,0:T(8,128)S(1)}, bf16[16,16,3072]{2,1,0:T(8,128)(2,1)}) fusion(f32[3072]{0:T(1024)S(1)} %copy-done, bf16[16,3072,256]{2,1,0:T(8,128)(2,1)} %param.4, bf16[16,16,256]{2,0,1:T(8,128)(2,1)S(1)} %pad_maximum_fusion), kind=kOutput, calls=%fused_computation.6 | convolution fusion | flops 405012480 | bytes 30027776 | tf_op jit(solution)/shard_map/fkc,fpc->fkp/dot_general | solution.py:106
  355.2 1.4 collective-permute-start.3
  356.6 34.3 %collective-permute-done.3 = bf16[16,16,3072]{2,1,0:T(8,128)(2,1)S(1)} collective-permute-done((bf16[16,16,3072]{2,1,0:T(8,128)(2,1)}, bf16[16,16,3072]{2,1,0:T(8,128)(2,1)S(1)}, u32[]{:S(2)}, u32[]{:S(2)}) %collective-permute-start.3) | collective-permute-done | bytes 1572896 | tf_op jit(solution)/shard_map/ppermute | solution.py:17
  390.8 1.3 collective-permute-start.4
  392.1 33.3 %collective-permute-done.4 = bf16[16,16,3072]{2,1,0:T(8,128)(2,1)S(1)} collective-permute-done((bf16[16,16,3072]{2,1,0:T(8,128)(2,1)S(1)}, bf16[16,16,3072]{2,1,0:T(8,128)(2,1)S(1)}, u32[]{:S(2)}, u32[]{:S(2)}) %collective-permute-start.4) | collective-permute-done | bytes 1572896 | tf_op jit(solution)/shard_map/ppermute | solution.py:17
  425.4 1.9 convolution_convert_fusion
  427.4 1.8 fusion.6
  429.2 1.8 fusion.4
  431.0 1.5 fusion.15
  432.5 1.8 fusion.21
  434.3 30.1 %psum.7 = f32[16,2,8,8]{3,2,0,1:T(8,128)S(1)} all-reduce(f32[16,2,8,8]{3,2,0,1:T(8,128)S(1)} %maximum_multiply_fusion.2), channel_id=1, replica_groups=mesh['freq'=4,'space'=8] {'space'}, use_global_device_ids=true, to_apply=%region_257.258 | all-reduce | flops 2048 | bytes 16384 | tf_op jit(solution)/shard_map/psum | solution.py:118
  464.4 0.7 copy.52
  (237 shorter events, 21.3 us)
Async XLA Ops:
  21.2 7.5 %collective-permute-start = (f32[16,256,256]{1,2,0:T(8,128)}, f32[16,256,256]{1,2,0:T(8,128)S(1)}, u32[]{:S(2)}, u32[]{:S(2)}) collective-permute-start(f32[16,256,256]{1,2,0:T(8,128)} %fusion.2), channel_id=1, source_target_pairs={{0,1},{1,0},{2,3},{3,2},{4,5},{5,4},{6,7},{7,6},{8,9},{9,8},{10,11... | collective-permute-start | bytes 12582920 | tf_op jit(solution)/shard_map/ppermute | solution.py:101
  31.8 93.9 %collective-permute-start.1 = (f32[16,256,256]{1,2,0:T(8,128)S(1)}, f32[16,256,256]{1,2,0:T(8,128)S(1)}, u32[]{:S(2)}, u32[]{:S(2)}) collective-permute-start(f32[16,256,256]{1,2,0:T(8,128)S(1)} %add.955), channel_id=1, source_target_pairs={{0,2},{1,3},{2,0},{3,1},{4,6},{5,7},{6,4},{7,5},{8,10},{9,11},{10,... | collective-permute-start | bytes 12582920 | tf_op jit(solution)/shard_map/ppermute | solution.py:101
  126.3 182.9 %collective-permute-start.2 = (f32[16,256,256]{1,2,0:T(8,128)S(1)}, f32[16,256,256]{1,2,0:T(8,128)S(1)}, u32[]{:S(2)}, u32[]{:S(2)}) collective-permute-start(f32[16,256,256]{1,2,0:T(8,128)S(1)} %add.956), channel_id=1, source_target_pairs={{0,4},{1,5},{2,6},{3,7},{4,0},{5,1},{6,2},{7,3},{8,12},{9,13},{10,... | collective-permute-start | bytes 12582920 | tf_op jit(solution)/shard_map/ppermute | solution.py:101
  338.7 3.9 copy-start.2
  340.2 2.6 copy-start
  342.6 12.6 %copy-start.1 = (f32[16,8]{0,1:T(8,128)}, f32[16,8]{0,1:T(8,128)S(1)}, u32[]{:S(2)}) copy-start(f32[16,8]{0,1:T(8,128)S(1)} %fusion.33) | copy-start | bytes 1540
  342.8 82.6 %copy-start.3 = (s32[16]{0:T(128)S(1)}, s32[16]{0:T(128)}, u32[]{:S(2)}) copy-start(s32[16]{0:T(128)} %param.6) | copy-start | bytes 196
  355.2 35.6 %collective-permute-start.3 = (bf16[16,16,3072]{2,1,0:T(8,128)(2,1)}, bf16[16,16,3072]{2,1,0:T(8,128)(2,1)S(1)}, u32[]{:S(2)}, u32[]{:S(2)}) collective-permute-start(bf16[16,16,3072]{2,1,0:T(8,128)(2,1)} %get-tuple-element.649), channel_id=1, source_target_pairs={{0,8},{8,0},{16,24},{24,16},{1,9},{9,1},{17,25},{25,17},{2,10},{10... | collective-permute-start | bytes 4718600 | tf_op jit(solution)/shard_map/ppermute | solution.py:17
  390.8 34.6 %collective-permute-start.4 = (bf16[16,16,3072]{2,1,0:T(8,128)(2,1)S(1)}, bf16[16,16,3072]{2,1,0:T(8,128)(2,1)S(1)}, u32[]{:S(2)}, u32[]{:S(2)}) collective-permute-start(bf16[16,16,3072]{2,1,0:T(8,128)(2,1)S(1)} %collective-permute-done.3), channel_id=1, source_target_pairs={{0,16},{16,0},{8,24},{24,8},{1,17},{17,1},{9,25},{25,9},{2,18},{18... | collective-permute-start | bytes 4718600 | tf_op jit(solution)/shard_map/ppermute | solution.py:17
